TPU v7x, 32 devices: a whole 2x2x4 slice. The times are simulated.
32 devices in a mesh: grp: 2 (over y), slab: 4 (over z), ang: 4 (over x, core).
Axes of the slice: x: 2, y: 2, z: 4, core: 2. Of those that a mesh axis runs over, the one named last changes fastest.
Arguments:
- volume: bfloat16 [16, 256, 1024], P(('grp', 'slab')), parts along dimension 0, may hold values from -6 to 6
- ray_weights: bfloat16 [8, 1024, 1024], P('ang'), may hold values from -0.0625 to 0.0625
- row_offsets: int32 [8, 8], P('ang'), may hold values from 0 to 8
- measured: float32 [16, 256, 1024], P(('grp', 'ang'), 'slab'), parts along dimension 0, may hold values from -6 to 6
- shifts: float32 [16], P(('grp', 'ang')), parts along dimension 0, may hold values from -4 to 4
Outputs:
- updated_volume: bfloat16 [16, 256, 1024], P(('grp', 'slab')), parts along dimension 0
- last_residual: float32 [16, 256, 1024], P(('grp', 'ang'), 'slab'), parts along dimension 0
- shift_slope: float32 [16], P(('grp', 'ang')), parts along dimension 0
There are 2 independent parts, one for each index of `grp`. A program takes and returns all parts, laid end to end along the dimension named above; an argument that names none is the same for every part. Nothing has to cross between parts.
All inputs are finite; a program needn't handle non-finite values.
Results may differ from a plain program's by a relative error of at most 0.006.
Values may be sent and summed in bfloat16 or wider, within the bound.
A program may use at most 128 MiB of HBM per device.

v0:
```python
import math
import jax
import jax.numpy as jnp
from jax import lax
from jax.sharding import PartitionSpec as P

Y = 256
X = 1024
U = 1024
OFF = 8
ROUNDS = 2
step_size = 0.5


def move_down(products, tilt_table):
    base = jnp.zeros((products.shape[1] + OFF, U), jnp.float32)
    placed = jax.vmap(
        lambda block, shift_rows: lax.dynamic_update_slice(base, block, (shift_rows, jnp.int32(0)))
    )(products, tilt_table)
    return jnp.sum(placed, axis=0)


def backproject(extended, tilt_table, ray_weights, band_rows):
    slices_count = tilt_table.shape[1]
    running = jnp.zeros((slices_count * band_rows, X), jnp.float32)
    for angle_index in range(ray_weights.shape[0]):
        source = extended[angle_index]
        picked = jax.vmap(
            lambda shift_rows: lax.dynamic_slice(source, (shift_rows, jnp.int32(0)), (band_rows, U))
        )(tilt_table[angle_index])
        running = running + lax.dot_general(
            picked.reshape(slices_count * band_rows, U),
            ray_weights[angle_index],
            (((1,), (1,)), ((), ())),
            preferred_element_type=jnp.float32,
        )
    return running


def apply_update(current, running):
    partial_value = lax.optimization_barrier(running.reshape(current.shape).astype(jnp.bfloat16))
    partial_wide = partial_value.astype(jnp.float32)
    gradient = lax.psum(partial_wide, "ang")
    renewed = (current.astype(jnp.float32) - step_size * gradient).astype(jnp.bfloat16)
    return renewed


def per_device(volume, ray_weights, row_offsets, measured, shifts):
    angles_here = ray_weights.shape[0]
    band_rows = measured.shape[1]
    highest = lax.Precision.HIGHEST
    numbers = lax.iota(jnp.int32, U)
    turns = numbers[:, None] * numbers[None, :] % U
    radians = turns.astype(jnp.float32) * (2.0 * math.pi / U)
    cosine = jnp.cos(radians)
    sine = jnp.sin(radians)
    signed = jnp.where(numbers <= (U - 1) // 2, numbers, numbers - U)
    omega = signed.astype(jnp.float32) * (2.0 * math.pi / U)
    flat_rows = measured.reshape(angles_here * band_rows, U)
    real_part = jnp.dot(flat_rows, cosine, precision=highest).reshape(angles_here, band_rows, U)
    imag_part = -jnp.dot(flat_rows, sine, precision=highest).reshape(angles_here, band_rows, U)
    phase = omega[None, None, :] * shifts[:, None, None]
    turned_real = real_part * jnp.cos(phase) + imag_part * jnp.sin(phase)
    turned_imag = imag_part * jnp.cos(phase) - real_part * jnp.sin(phase)
    first_half = jnp.concatenate([turned_real, omega * turned_imag], axis=0).reshape(-1, U)
    second_half = jnp.concatenate([turned_imag, -omega * turned_real], axis=0).reshape(-1, U)
    inverse = (
        jnp.dot(first_half, cosine, precision=highest)
        - jnp.dot(second_half, sine, precision=highest)
    ) / U
    inverse = inverse.reshape(2, angles_here, band_rows, U)
    shifted = inverse[0]
    slope_field = inverse[1]
    projection = shifted
    residual = shifted
    current = volume
    slices_here = volume.shape[0]
    tilt_table = lax.dynamic_slice_in_dim(
        row_offsets, lax.axis_index("slab") * slices_here, slices_here, 1
    )
    for round_index in range(ROUNDS):
        flattened = current.reshape(slices_here * Y, X)
        partials = jnp.stack(
            [
                move_down(
                    jnp.dot(
                        flattened, ray_weights[angle_index], preferred_element_type=jnp.float32
                    ).reshape(slices_here, Y, U),
                    tilt_table[angle_index],
                )[:Y]
                for angle_index in range(angles_here)
            ]
        )
        projection = lax.psum_scatter(partials, "slab", scatter_dimension=1, tiled=True)
        residual = projection - shifted
        rounded = residual.astype(jnp.bfloat16)
        gathered = lax.all_gather(rounded, "slab", axis=1, tiled=True)
        extended = jnp.concatenate(
            [gathered, jnp.zeros((angles_here, OFF, U), jnp.bfloat16)], axis=1
        )
        running = backproject(extended, tilt_table, ray_weights, Y)
        current = apply_update(current, running)
    local_dot = jnp.sum(projection * slope_field, axis=(1, 2))
    shift_slope = lax.psum(local_dot, "slab") / math.sqrt(Y * U)
    return (current, residual, shift_slope)


def solution(mesh):
    in_specs = (
        P(("grp", "slab"), None, None),
        P("ang", None, None),
        P("ang", None),
        P(("grp", "ang"), "slab", None),
        P(("grp", "ang")),
    )
    out_specs = (P(("grp", "slab"), None, None), P(("grp", "ang"), "slab", None), P(("grp", "ang")))
    return jax.shard_map(
        per_device, mesh=mesh, in_specs=in_specs, out_specs=out_specs, check_vma=False
    )
```

profile of v0, /device:TPU:1, one launch (start us, length us, event | category | flops | bytes accessed | tf_op | source)
XLA Modules:
  0.0 434.2 jit_solution(13662559025870306911)
XLA Ops:
  7.3 4.6 %fusion.16 = f32[2,256,1024]{2,1,0:T(8,128)} fusion(bf16[2,256,1024]{2,1,0:T(8,128)(2,1)} %param.5, bf16[2,1024,1024]{2,1,0:T(8,128)(2,1)} %param.6), kind=kOutput, calls=%fused_computation.41 | convolution fusion | flops 1073741824 | bytes 5242880 | tf_op jit(solution)/shard_map/dot_general | solution.py:86
  11.9 2.6 fusion.8
  16.4 23.4 %while.12 = (s32[]{:T(128)}, f32[2,264,1024]{2,1,0:T(8,128)}, s32[2,3]{1,0:T(2,128)S(1)}, f32[2,256,1024]{2,1,0:T(8,128)}, s32[]{:T(128)}, /*index=5*/s32[3]{0:T(128)S(1)}, s32[]{:T(128)}) while((s32[]{:T(128)}, f32[2,264,1024]{2,1,0:T(8,128)}, s32[2,3]{1,0:T(2,128)S(1)}, f32[2,256,1024]{2,1,0:T(8,128)}, s32[]{:T(128)}, /*index=5*/s32[3]{0:T(128)S(1)}, ...), condition=%wide.while_cond.4, body=%wide.while_body.4.sunk | while | flops 262163 | bytes 5243051 | solution.py:18
  17.0 2.6 and_reduce_fusion.8
  19.6 3.6 dynamic-slice_select_fusion.8
  23.2 4.9 %dynamic-update-slice.32 = f32[2,264,1024]{2,1,0:T(8,128)} dynamic-update-slice(f32[2,264,1024]{2,1,0:T(8,128)} %get-tuple-element.455, f32[1,256,1024]{2,1,0:T(8,128)S(1)} %dynamic-slice_select_fusion.8, s32[]{:T(128)} %bitcast.154, s32[]{:T(128)} %bitcast.155, s32[]{:T(128)} %constant.18.clone.1..sunk) | dynamic-update-slice | bytes 2097156 | tf_op jit(solution)/shard_map/vmap(vmap())/scatter
  28.7 2.6 and_reduce_fusion.8
  31.3 3.6 dynamic-slice_select_fusion.8
  34.9 4.9 %dynamic-update-slice.32 = f32[2,264,1024]{2,1,0:T(8,128)} dynamic-update-slice(f32[2,264,1024]{2,1,0:T(8,128)} %get-tuple-element.455, f32[1,256,1024]{2,1,0:T(8,128)S(1)} %dynamic-slice_select_fusion.8, s32[]{:T(128)} %bitcast.154, s32[]{:T(128)} %bitcast.155, s32[]{:T(128)} %constant.18.clone.1..sunk) | dynamic-update-slice | bytes 2097156 | tf_op jit(solution)/shard_map/vmap(vmap())/scatter
  41.5 23.9 %while.13 = (s32[]{:T(128)}, f32[2,264,1024]{2,1,0:T(8,128)}, s32[2,3]{1,0:T(2,128)S(1)}, f32[2,256,1024]{2,1,0:T(8,128)}, s32[]{:T(128)}, /*index=5*/s32[3]{0:T(128)S(1)}, s32[]{:T(128)}) while((s32[]{:T(128)}, f32[2,264,1024]{2,1,0:T(8,128)}, s32[2,3]{1,0:T(2,128)S(1)}, f32[2,256,1024]{2,1,0:T(8,128)}, s32[]{:T(128)}, /*index=5*/s32[3]{0:T(128)S(1)}, ...), condition=%wide.while_cond.5, body=%wide.while_body.5.sunk | while | flops 262163 | bytes 5243051 | solution.py:18
  42.2 2.7 and_reduce_fusion.9
  44.9 3.7 dynamic-slice_select_fusion.9
  48.6 5.0 %dynamic-update-slice.33 = f32[2,264,1024]{2,1,0:T(8,128)} dynamic-update-slice(f32[2,264,1024]{2,1,0:T(8,128)} %get-tuple-element.434, f32[1,256,1024]{2,1,0:T(8,128)S(1)} %dynamic-slice_select_fusion.9, s32[]{:T(128)} %bitcast.159, s32[]{:T(128)} %bitcast.160, s32[]{:T(128)} %constant.18.clone.1..sunk.1) | dynamic-update-slice | bytes 2097156 | tf_op jit(solution)/shard_map/vmap(vmap())/scatter
  54.3 2.7 and_reduce_fusion.9
  57.0 3.7 dynamic-slice_select_fusion.9
  60.7 4.8 %dynamic-update-slice.33 = f32[2,264,1024]{2,1,0:T(8,128)} dynamic-update-slice(f32[2,264,1024]{2,1,0:T(8,128)} %get-tuple-element.434, f32[1,256,1024]{2,1,0:T(8,128)S(1)} %dynamic-slice_select_fusion.9, s32[]{:T(128)} %bitcast.159, s32[]{:T(128)} %bitcast.160, s32[]{:T(128)} %constant.18.clone.1..sunk.1) | dynamic-update-slice | bytes 2097156 | tf_op jit(solution)/shard_map/vmap(vmap())/scatter
  65.4 3.0 reduce_sum.45
  73.6 18.6 %fusion.26 = f32[1024,128]{0,1:T(8,128)S(1)} fusion(f32[128,1024]{1,0:T(8,128)S(1)} %bitcast.174), kind=kOutput, calls=%fused_computation.54 | convolution fusion | flops 1625292800 | bytes 1048576 | tf_op jit(solution)/shard_map/dot_general | solution.py:60
  92.2 18.7 %fusion.50 = f32[1024,128]{0,1:T(8,128)S(1)} fusion(f32[128,1024]{1,0:T(8,128)S(1)} %bitcast.175), kind=kOutput, calls=%fused_computation.67 | convolution fusion | flops 1625423872 | bytes 1048576 | tf_op jit(solution)/shard_map/dot_general | solution.py:61
  111.3 20.2 %fusion.24 = f32[256,1024]{1,0:T(8,128)S(1)} fusion(f32[256,1024]{1,0:T(8,128)S(1)} %bitcast.185), kind=kOutput, calls=%fused_computation.53 | convolution fusion | flops 3235905536 | bytes 2097152 | tf_op jit(solution)/shard_map/dot_general | solution.py:68
  131.5 20.1 %fusion.47 = f32[256,1024]{1,0:T(8,128)S(1)} fusion(f32[256,1024]{1,0:T(8,128)S(1)} %fusion.24, f32[256,1024]{1,0:T(8,128)S(1)} %bitcast.184), kind=kOutput, calls=%fused_computation.66 | convolution fusion | flops 3236429824 | bytes 3145728 | tf_op jit(solution)/shard_map/dot_general | solution.py:69
  153.8 29.5 %all-gather.3.cloned.1.call-done = bf16[2,256,1024]{2,1,0:T(8,128)(2,1)} async-done(((bf16[2,64,1024]{2,1,0:T(8,128)(2,1)}), bf16[2,256,1024]{2,1,0:T(8,128)(2,1)}) %all-gather.3.cloned.1.call-update) | async-done | bytes 1048592 | tf_op jit(solution)/shard_map/all_gather | solution.py:97
  185.3 4.2 fusion.10
  190.1 4.5 %add_convert_fusion.1 = bf16[512,1024]{1,0:T(8,128)(2,1)} fusion(f32[512,1024]{1,0:T(8,128)} %fusion.10, bf16[512,1024]{1,0:T(8,128)(2,1)S(1)} %bitcast.182, bf16[2,1024,1024]{2,1,0:T(8,128)(2,1)} %param.6), kind=kOutput, calls=%fused_computation.50 | convolution fusion | flops 1074790400 | bytes 6291456 | tf_op jit(solution)/shard_map/dot_general | solution.py:31
  194.6 42.1 %all-reduce.6 = f32[2,256,1024]{2,1,0:T(8,128)S(1)} all-reduce(bf16[2,256,1024]{2,1,0:T(8,128)(2,1)} %bitcast.178), channel_id=1, replica_groups=mesh['grp'=2,'slab'=4,'ang'=4] {'ang'}, use_global_device_ids=true, to_apply=%region_5.6 | all-reduce | flops 524288 | bytes 3145728 | tf_op jit(solution)/shard_map/psum | solution.py:43
  239.1 2.6 fusion.14
  241.7 2.6 fusion.6
  245.9 23.4 %while.14 = (s32[]{:T(128)}, f32[2,264,1024]{2,1,0:T(8,128)}, s32[2,3]{1,0:T(2,128)S(1)}, f32[2,256,1024]{2,1,0:T(8,128)}, s32[]{:T(128)}, /*index=5*/s32[3]{0:T(128)S(1)}, s32[]{:T(128)}) while((s32[]{:T(128)}, f32[2,264,1024]{2,1,0:T(8,128)}, s32[2,3]{1,0:T(2,128)S(1)}, f32[2,256,1024]{2,1,0:T(8,128)}, s32[]{:T(128)}, /*index=5*/s32[3]{0:T(128)S(1)}, ...), condition=%wide.while_cond.6, body=%wide.while_body.6.sunk | while | flops 262163 | bytes 5243051 | solution.py:18
  246.5 2.6 and_reduce_fusion.10
  249.1 3.5 dynamic-slice_select_fusion.10
  252.7 5.0 %dynamic-update-slice.34 = f32[2,264,1024]{2,1,0:T(8,128)} dynamic-update-slice(f32[2,264,1024]{2,1,0:T(8,128)} %get-tuple-element.527, f32[1,256,1024]{2,1,0:T(8,128)S(1)} %dynamic-slice_select_fusion.10, s32[]{:T(128)} %bitcast.164, s32[]{:T(128)} %bitcast.165, s32[]{:T(128)} %constant.18.clone.1..sunk.2) | dynamic-update-slice | bytes 2097156 | tf_op jit(solution)/shard_map/vmap(vmap())/scatter
  258.3 2.6 and_reduce_fusion.10
  260.9 3.5 dynamic-slice_select_fusion.10
  264.4 5.0 %dynamic-update-slice.34 = f32[2,264,1024]{2,1,0:T(8,128)} dynamic-update-slice(f32[2,264,1024]{2,1,0:T(8,128)} %get-tuple-element.527, f32[1,256,1024]{2,1,0:T(8,128)S(1)} %dynamic-slice_select_fusion.10, s32[]{:T(128)} %bitcast.164, s32[]{:T(128)} %bitcast.165, s32[]{:T(128)} %constant.18.clone.1..sunk.2) | dynamic-update-slice | bytes 2097156 | tf_op jit(solution)/shard_map/vmap(vmap())/scatter
  273.0 23.3 %while.15 = (s32[]{:T(128)}, f32[2,264,1024]{2,1,0:T(8,128)}, s32[2,3]{1,0:T(2,128)S(1)}, f32[2,256,1024]{2,1,0:T(8,128)}, s32[]{:T(128)}, /*index=5*/s32[3]{0:T(128)S(1)}, s32[]{:T(128)}) while((s32[]{:T(128)}, f32[2,264,1024]{2,1,0:T(8,128)}, s32[2,3]{1,0:T(2,128)S(1)}, f32[2,256,1024]{2,1,0:T(8,128)}, s32[]{:T(128)}, /*index=5*/s32[3]{0:T(128)S(1)}, ...), condition=%wide.while_cond.7, body=%wide.while_body.7.sunk | while | flops 262163 | bytes 5243051 | solution.py:18
  273.6 2.6 and_reduce_fusion.11
  276.2 3.6 dynamic-slice_select_fusion.11
  279.8 5.0 %dynamic-update-slice.35 = f32[2,264,1024]{2,1,0:T(8,128)} dynamic-update-slice(f32[2,264,1024]{2,1,0:T(8,128)} %get-tuple-element.506, f32[1,256,1024]{2,1,0:T(8,128)S(1)} %dynamic-slice_select_fusion.11, s32[]{:T(128)} %bitcast.169, s32[]{:T(128)} %bitcast.170, s32[]{:T(128)} %constant.18.clone.1..sunk.3) | dynamic-update-slice | bytes 2097156 | tf_op jit(solution)/shard_map/vmap(vmap())/scatter
  285.4 2.6 and_reduce_fusion.11
  288.0 3.5 dynamic-slice_select_fusion.11
  291.5 4.7 %dynamic-update-slice.35 = f32[2,264,1024]{2,1,0:T(8,128)} dynamic-update-slice(f32[2,264,1024]{2,1,0:T(8,128)} %get-tuple-element.506, f32[1,256,1024]{2,1,0:T(8,128)S(1)} %dynamic-slice_select_fusion.11, s32[]{:T(128)} %bitcast.169, s32[]{:T(128)} %bitcast.170, s32[]{:T(128)} %constant.18.clone.1..sunk.3) | dynamic-update-slice | bytes 2097156 | tf_op jit(solution)/shard_map/vmap(vmap())/scatter
  299.9 42.4 %reduce-scatter.5.cloned.1.call-done = f32[2,64,1024]{2,1,0:T(8,128)} async-done(((f32[2,256,1024]{2,1,0:T(8,128)}), f32[2,64,1024]{2,1,0:T(8,128)}) %reduce-scatter.5.cloned.1.call-update) | async-done | bytes 524304 | tf_op jit(solution)/shard_map/reduce_scatter | solution.py:94
  344.4 8.7 %psum.23 = f32[2]{0:T(128)S(1)} all-reduce(f32[2]{0:T(128)S(1)} %get-tuple-element.189), channel_id=1, replica_groups=mesh['grp'=2,'slab'=4,'ang'=4] {'slab'}, use_global_device_ids=true, to_apply=%region_13.14 | all-reduce | flops 2 | bytes 16 | tf_op jit(solution)/shard_map/psum | solution.py:104
  353.6 18.1 %all-gather.5.cloned.1.call-done = bf16[2,256,1024]{2,1,0:T(8,128)(2,1)} async-done(((bf16[2,64,1024]{2,1,0:T(8,128)(2,1)}), bf16[2,256,1024]{2,1,0:T(8,128)(2,1)}) %all-gather.5.cloned.1.call-update) | async-done | bytes 1048592 | tf_op jit(solution)/shard_map/all_gather | solution.py:97
  373.5 4.2 fusion.12
  378.2 4.5 %add_convert_fusion = bf16[512,1024]{1,0:T(8,128)(2,1)} fusion(f32[512,1024]{1,0:T(8,128)} %fusion.12, bf16[512,1024]{1,0:T(8,128)(2,1)S(1)} %bitcast.180, bf16[2,1024,1024]{2,1,0:T(8,128)(2,1)} %param.6), kind=kOutput, calls=%fused_computation.48 | convolution fusion | flops 1074790400 | bytes 6291456 | tf_op jit(solution)/shard_map/dot_general | solution.py:31
  382.7 42.2 %all-reduce.7 = f32[2,256,1024]{2,1,0:T(8,128)S(1)} all-reduce(bf16[2,256,1024]{2,1,0:T(8,128)(2,1)} %bitcast.179), channel_id=1, replica_groups=mesh['grp'=2,'slab'=4,'ang'=4] {'ang'}, use_global_device_ids=true, to_apply=%region_11.12 | all-reduce | flops 524288 | bytes 3145728 | tf_op jit(solution)/shard_map/psum | solution.py:43
  424.9 2.6 subtract_convert_fusion
  (106 shorter events, 36.6 us)
Async XLA Ops:
  7.2 66.5 %copy-start = (f32[2,64,1024]{2,1,0:T(8,128)S(1)}, f32[2,64,1024]{2,1,0:T(8,128)}, u32[]{:S(2)}) copy-start(f32[2,64,1024]{2,1,0:T(8,128)} %param.8) | copy-start | bytes 1572868
  7.2 144.5 %reduce-scatter.3.cloned.1.call-start = ((), (), s32[]{:S(2)}) async-start(), calls=%async_computation.2 | async-start | bytes 2621440 | tf_op jit(solution)/shard_map/reduce_scatter | solution.py:94
  7.2 4.7 %copy-start.4 = (bf16[2,256,1024]{2,1,0:T(8,128)(2,1)S(1)}, bf16[2,256,1024]{2,1,0:T(8,128)(2,1)}, u32[]{:S(2)}) copy-start(bf16[2,256,1024]{2,1,0:T(8,128)(2,1)} %param.5) | copy-start | bytes 3145732
  7.2 4.7 %copy-start.9 = (bf16[2,1024,1024]{2,1,0:T(8,128)(2,1)S(1)}, bf16[2,1024,1024]{2,1,0:T(8,128)(2,1)}, u32[]{:S(2)}) copy-start(bf16[2,1024,1024]{2,1,0:T(8,128)(2,1)} %param.6) | copy-start | bytes 12582916
  11.9 2.6 copy-start.6
  11.9 2.7 copy-start.7
  14.5 1.9 copy-start.5
  65.4 3.0 copy-start.2
  71.4 2.0 copy-start.8
  72.9 110.4 %all-gather.3.cloned.1.call-start = ((), (), s32[]{:S(2)}) async-start(), calls=%async_computation.3 | async-start | bytes 1310720 | tf_op jit(solution)/shard_map/all_gather | solution.py:97
  153.6 188.7 %reduce-scatter.5.cloned.1.call-start = ((), (), s32[]{:S(2)}) async-start(), calls=%async_computation.4 | async-start | bytes 2621440 | tf_op jit(solution)/shard_map/reduce_scatter | solution.py:94
  236.6 2.5 copy-start.10
  239.1 2.6 copy-start.3
  299.8 71.8 %all-gather.5.cloned.1.call-start = ((), (), s32[]{:S(2)}) async-start(), calls=%async_computation.5 | async-start | bytes 1310720 | tf_op jit(solution)/shard_map/all_gather | solution.py:97
  382.7 44.7 %copy-start.1 = (f32[2,64,1024]{2,1,0:T(8,128)S(1)}, f32[2,64,1024]{2,1,0:T(8,128)}, u32[]{:S(2)}) copy-start(f32[2,64,1024]{2,1,0:T(8,128)} %param.8) | copy-start | bytes 1572868
Sparse Core Ops, SparseCore 0:
  73.0 45.3 reduce-scatter.2
  153.7 29.5 all-gather.2
  299.9 42.2 reduce-scatter.4
  344.5 27.0 all-gather.4
where the time goes:
time: 440 us; the launch traced here: 434 us
  matrix products  107 us (24%)
  blocking collectives  92.9 us (21%)
  waiting for transfers between devices  90 us (20%)
  other arithmetic  70.2 us (16%)
  local copies, waits for them, and re-layouts  58.4 us (13%)
  between operations  14.3 us (3%)
    psum x2, blocking collectives, apply_update(): gradient = lax.psum(partial_wide, 'ang')  84.2 us
    scatter x16, other arithmetic  49.8 us
    all_gather x2, waiting for transfers between devices, per_device(): gathered = lax.all_gather(rounded, 'slab', axis=1, tiled=True)  47.5 us
    scatter x24, local copies, waits for them, and re-layouts  44.2 us
    reduce_scatter x2, waiting for transfers between devices, per_device(): lax.psum_scatter(partials, 'slab', scatter_dimension=1, tiled=True)  42.4 us
    dot_general x1, matrix products, per_device(): jnp.dot(first_half, cosine, precision=highest)  20.2 us
    dot_general x1, matrix products, per_device(): jnp.dot(second_half, sine, precision=highest)  20.1 us
    dot_general x1, matrix products, per_device(): jnp.dot(flat_rows, sine, precision=highest)  18.7 us
  transfers between devices with their start and end apart: 4, of which 3 were waited for; matrix products, arithmetic and copies ran while one was open for 18% of the time, Pallas kernels for 0%

commit v1 on v0

--- a/solution.py
+++ b/solution.py
@@ -40,7 +40,9 @@
 def apply_update(current, running):
     partial_value = lax.optimization_barrier(running.reshape(current.shape).astype(jnp.bfloat16))
     partial_wide = partial_value.astype(jnp.float32)
-    gradient = lax.psum(partial_wide, "ang")
+    gradient = partial_wide
+    for hop in (1, 2):
+        gradient = gradient + lax.ppermute(gradient, "ang", [(dev, dev ^ hop) for dev in range(4)])
     renewed = (current.astype(jnp.float32) - step_size * gradient).astype(jnp.bfloat16)
     return renewed
 

time: 440 us -> 463 us (1.052)
  waiting for transfers between devices: 90 us -> 191 us
  blocking collectives: 92.9 us -> 8.1 us
  starting transfers between devices: 0.63 us -> 5.56 us
    ppermute x0 -> x4, waiting for transfers between devices: none -> 90.4 us  [apply_update(): lax.ppermute(gradient, 'ang', [(dev, dev ^ hop) for dev in range(4)])]
    psum x2 -> x0, blocking collectives: 84.2 us -> none  [apply_update(): gradient = lax.psum(partial_wide, 'ang')]
    all_gather x2, waiting for transfers between devices: 47.5 us -> 56.7 us  [per_device(): gathered = lax.all_gather(rounded, 'slab', axis=1, tiled=True)]
    ppermute x0 -> x4, starting transfers between devices: none -> 4.93 us  [apply_update(): lax.ppermute(gradient, 'ang', [(dev, dev ^ hop) for dev in range(4)])]
  transfers between devices with their start and end apart: 4 -> 8, of which waited for: 3 -> 7; matrix products, arithmetic and copies ran while one was open for 18% -> 17% of each run, Pallas kernels for 0% -> 0%
where the time goes in v1:
time: 463 us; the launch traced here: 456 us
  waiting for transfers between devices  191 us (41%)
  matrix products  105 us (23%)
  other arithmetic  73.7 us (16%)
  local copies, waits for them, and re-layouts  57.9 us (13%)
  between operations  14.3 us (3%)
  blocking collectives  8.1 us (2%)
  starting transfers between devices  5.56 us (1%)
    ppermute x4, waiting for transfers between devices, apply_update(): lax.ppermute(gradient, 'ang', [(dev, dev ^ hop) for dev in range(4)])  90.4 us
    all_gather x2, waiting for transfers between devices, per_device(): gathered = lax.all_gather(rounded, 'slab', axis=1, tiled=True)  56.7 us
    scatter x16, other arithmetic  50.4 us
    scatter x24, local copies, waits for them, and re-layouts  44.4 us
    reduce_scatter x2, waiting for transfers between devices, per_device(): lax.psum_scatter(partials, 'slab', scatter_dimension=1, tiled=True)  43.6 us
    dot_general x1, matrix products, per_device(): jnp.dot(first_half, cosine, precision=highest)  20.2 us
    dot_general x1, matrix products, per_device(): jnp.dot(second_half, sine, precision=highest)  20.1 us
    dot_general x1, matrix products, per_device(): jnp.dot(flat_rows, sine, precision=highest)  18.7 us
  transfers between devices with their start and end apart: 8, of which 7 were waited for; matrix products, arithmetic and copies ran while one was open for 17% of the time, Pallas kernels for 0%

profile of v1, /device:TPU:1, one launch (start us, length us, event | category | flops | bytes accessed | tf_op | source)
XLA Modules:
  0.0 456.2 jit_solution(10557271269738979472)
XLA Ops:
  7.3 4.6 %fusion.16 = f32[2,256,1024]{2,1,0:T(8,128)} fusion(bf16[2,256,1024]{2,1,0:T(8,128)(2,1)} %param.5, bf16[2,1024,1024]{2,1,0:T(8,128)(2,1)} %param.6), kind=kOutput, calls=%fused_computation.41 | convolution fusion | flops 1073741824 | bytes 5242880 | tf_op jit(solution)/shard_map/dot_general | solution.py:88
  11.9 2.6 fusion.8
  16.4 23.3 %while.12 = (s32[]{:T(128)}, f32[2,264,1024]{2,1,0:T(8,128)}, s32[2,3]{1,0:T(2,128)S(1)}, f32[2,256,1024]{2,1,0:T(8,128)}, s32[]{:T(128)}, /*index=5*/s32[3]{0:T(128)S(1)}, s32[]{:T(128)}) while((s32[]{:T(128)}, f32[2,264,1024]{2,1,0:T(8,128)}, s32[2,3]{1,0:T(2,128)S(1)}, f32[2,256,1024]{2,1,0:T(8,128)}, s32[]{:T(128)}, /*index=5*/s32[3]{0:T(128)S(1)}, ...), condition=%wide.while_cond.4, body=%wide.while_body.4.sunk | while | flops 262163 | bytes 5243051 | solution.py:18
  19.6 3.6 dynamic-slice_select_fusion.8
  23.2 4.9 %dynamic-update-slice.32 = f32[2,264,1024]{2,1,0:T(8,128)} dynamic-update-slice(f32[2,264,1024]{2,1,0:T(8,128)} %get-tuple-element.455, f32[1,256,1024]{2,1,0:T(8,128)S(1)} %dynamic-slice_select_fusion.8, s32[]{:T(128)} %bitcast.154, s32[]{:T(128)} %bitcast.155, s32[]{:T(128)} %constant.18.clone.1..sunk) | dynamic-update-slice | bytes 2097156 | tf_op jit(solution)/shard_map/vmap(vmap())/scatter
  31.3 3.6 dynamic-slice_select_fusion.8
  34.8 4.9 %dynamic-update-slice.32 = f32[2,264,1024]{2,1,0:T(8,128)} dynamic-update-slice(f32[2,264,1024]{2,1,0:T(8,128)} %get-tuple-element.455, f32[1,256,1024]{2,1,0:T(8,128)S(1)} %dynamic-slice_select_fusion.8, s32[]{:T(128)} %bitcast.154, s32[]{:T(128)} %bitcast.155, s32[]{:T(128)} %constant.18.clone.1..sunk) | dynamic-update-slice | bytes 2097156 | tf_op jit(solution)/shard_map/vmap(vmap())/scatter
  41.4 24.2 %while.13 = (s32[]{:T(128)}, f32[2,264,1024]{2,1,0:T(8,128)}, s32[2,3]{1,0:T(2,128)S(1)}, f32[2,256,1024]{2,1,0:T(8,128)}, s32[]{:T(128)}, /*index=5*/s32[3]{0:T(128)S(1)}, s32[]{:T(128)}) while((s32[]{:T(128)}, f32[2,264,1024]{2,1,0:T(8,128)}, s32[2,3]{1,0:T(2,128)S(1)}, f32[2,256,1024]{2,1,0:T(8,128)}, s32[]{:T(128)}, /*index=5*/s32[3]{0:T(128)S(1)}, ...), condition=%wide.while_cond.5, body=%wide.while_body.5.sunk | while | flops 262163 | bytes 5243051 | solution.py:18
  42.1 2.7 and_reduce_fusion.9
  44.8 3.7 dynamic-slice_select_fusion.9
  48.6 5.1 %dynamic-update-slice.33 = f32[2,264,1024]{2,1,0:T(8,128)} dynamic-update-slice(f32[2,264,1024]{2,1,0:T(8,128)} %get-tuple-element.434, f32[1,256,1024]{2,1,0:T(8,128)S(1)} %dynamic-slice_select_fusion.9, s32[]{:T(128)} %bitcast.159, s32[]{:T(128)} %bitcast.160, s32[]{:T(128)} %constant.18.clone.1..sunk.1) | dynamic-update-slice | bytes 2097156 | tf_op jit(solution)/shard_map/vmap(vmap())/scatter
  54.3 2.7 and_reduce_fusion.9
  57.1 3.7 dynamic-slice_select_fusion.9
  60.8 4.8 %dynamic-update-slice.33 = f32[2,264,1024]{2,1,0:T(8,128)} dynamic-update-slice(f32[2,264,1024]{2,1,0:T(8,128)} %get-tuple-element.434, f32[1,256,1024]{2,1,0:T(8,128)S(1)} %dynamic-slice_select_fusion.9, s32[]{:T(128)} %bitcast.159, s32[]{:T(128)} %bitcast.160, s32[]{:T(128)} %constant.18.clone.1..sunk.1) | dynamic-update-slice | bytes 2097156 | tf_op jit(solution)/shard_map/vmap(vmap())/scatter
  65.6 3.0 reduce_sum.45
  73.9 18.6 %fusion.26 = f32[1024,128]{0,1:T(8,128)S(1)} fusion(f32[128,1024]{1,0:T(8,128)S(1)} %bitcast.174), kind=kOutput, calls=%fused_computation.54 | convolution fusion | flops 1625292800 | bytes 1048576 | tf_op jit(solution)/shard_map/dot_general | solution.py:62
  92.5 18.7 %fusion.50 = f32[1024,128]{0,1:T(8,128)S(1)} fusion(f32[128,1024]{1,0:T(8,128)S(1)} %bitcast.175), kind=kOutput, calls=%fused_computation.67 | convolution fusion | flops 1625423872 | bytes 1048576 | tf_op jit(solution)/shard_map/dot_general | solution.py:63
  111.5 20.2 %fusion.24 = f32[256,1024]{1,0:T(8,128)S(1)} fusion(f32[256,1024]{1,0:T(8,128)S(1)} %bitcast.187), kind=kOutput, calls=%fused_computation.53 | convolution fusion | flops 3235905536 | bytes 2097152 | tf_op jit(solution)/shard_map/dot_general | solution.py:70
  131.7 20.1 %fusion.47 = f32[256,1024]{1,0:T(8,128)S(1)} fusion(f32[256,1024]{1,0:T(8,128)S(1)} %fusion.24, f32[256,1024]{1,0:T(8,128)S(1)} %bitcast.186), kind=kOutput, calls=%fused_computation.66 | convolution fusion | flops 3236429824 | bytes 3145728 | tf_op jit(solution)/shard_map/dot_general | solution.py:71
  154.0 29.4 %all-gather.3.cloned.1.call-done = bf16[2,256,1024]{2,1,0:T(8,128)(2,1)} async-done(((bf16[2,64,1024]{2,1,0:T(8,128)(2,1)}), bf16[2,256,1024]{2,1,0:T(8,128)(2,1)}) %all-gather.3.cloned.1.call-update) | async-done | bytes 1048592 | tf_op jit(solution)/shard_map/all_gather | solution.py:99
  185.5 4.2 fusion.10
  190.3 3.5 add_convert_fusion.1
  195.3 3.8 collective-permute-done
  200.7 45.7 %collective-permute-done.1 = f32[2,256,1024]{2,1,0:T(8,128)} collective-permute-done((f32[2,256,1024]{2,1,0:T(8,128)S(1)}, f32[2,256,1024]{2,1,0:T(8,128)}, u32[]{:S(2)}, u32[]{:S(2)}) %collective-permute-start.1) | collective-permute-done | bytes 2097184 | tf_op jit(solution)/shard_map/ppermute | solution.py:45
  248.9 2.6 fusion.14
  251.5 2.6 fusion.6
  255.7 23.7 %while.14 = (s32[]{:T(128)}, f32[2,264,1024]{2,1,0:T(8,128)}, s32[2,3]{1,0:T(2,128)S(1)}, f32[2,256,1024]{2,1,0:T(8,128)}, s32[]{:T(128)}, /*index=5*/s32[3]{0:T(128)S(1)}, s32[]{:T(128)}) while((s32[]{:T(128)}, f32[2,264,1024]{2,1,0:T(8,128)}, s32[2,3]{1,0:T(2,128)S(1)}, f32[2,256,1024]{2,1,0:T(8,128)}, s32[]{:T(128)}, /*index=5*/s32[3]{0:T(128)S(1)}, ...), condition=%wide.while_cond.6, body=%wide.while_body.6.sunk | while | flops 262163 | bytes 5243051 | solution.py:18
  256.3 2.6 and_reduce_fusion.10
  258.9 3.7 dynamic-slice_select_fusion.10
  262.6 5.0 %dynamic-update-slice.34 = f32[2,264,1024]{2,1,0:T(8,128)} dynamic-update-slice(f32[2,264,1024]{2,1,0:T(8,128)} %get-tuple-element.527, f32[1,256,1024]{2,1,0:T(8,128)S(1)} %dynamic-slice_select_fusion.10, s32[]{:T(128)} %bitcast.164, s32[]{:T(128)} %bitcast.165, s32[]{:T(128)} %constant.18.clone.1..sunk.2) | dynamic-update-slice | bytes 2097156 | tf_op jit(solution)/shard_map/vmap(vmap())/scatter
  268.2 2.6 and_reduce_fusion.10
  270.8 3.7 dynamic-slice_select_fusion.10
  274.5 5.0 %dynamic-update-slice.34 = f32[2,264,1024]{2,1,0:T(8,128)} dynamic-update-slice(f32[2,264,1024]{2,1,0:T(8,128)} %get-tuple-element.527, f32[1,256,1024]{2,1,0:T(8,128)S(1)} %dynamic-slice_select_fusion.10, s32[]{:T(128)} %bitcast.164, s32[]{:T(128)} %bitcast.165, s32[]{:T(128)} %constant.18.clone.1..sunk.2) | dynamic-update-slice | bytes 2097156 | tf_op jit(solution)/shard_map/vmap(vmap())/scatter
  283.1 23.7 %while.15 = (s32[]{:T(128)}, f32[2,264,1024]{2,1,0:T(8,128)}, s32[2,3]{1,0:T(2,128)S(1)}, f32[2,256,1024]{2,1,0:T(8,128)}, s32[]{:T(128)}, /*index=5*/s32[3]{0:T(128)S(1)}, s32[]{:T(128)}) while((s32[]{:T(128)}, f32[2,264,1024]{2,1,0:T(8,128)}, s32[2,3]{1,0:T(2,128)S(1)}, f32[2,256,1024]{2,1,0:T(8,128)}, s32[]{:T(128)}, /*index=5*/s32[3]{0:T(128)S(1)}, ...), condition=%wide.while_cond.7, body=%wide.while_body.7.sunk | while | flops 262163 | bytes 5243051 | solution.py:18
  283.8 2.7 and_reduce_fusion.11
  286.4 3.7 dynamic-slice_select_fusion.11
  290.1 5.0 %dynamic-update-slice.35 = f32[2,264,1024]{2,1,0:T(8,128)} dynamic-update-slice(f32[2,264,1024]{2,1,0:T(8,128)} %get-tuple-element.506, f32[1,256,1024]{2,1,0:T(8,128)S(1)} %dynamic-slice_select_fusion.11, s32[]{:T(128)} %bitcast.169, s32[]{:T(128)} %bitcast.170, s32[]{:T(128)} %constant.18.clone.1..sunk.3) | dynamic-update-slice | bytes 2097156 | tf_op jit(solution)/shard_map/vmap(vmap())/scatter
  295.7 2.7 and_reduce_fusion.11
  298.4 3.7 dynamic-slice_select_fusion.11
  302.0 4.7 %dynamic-update-slice.35 = f32[2,264,1024]{2,1,0:T(8,128)} dynamic-update-slice(f32[2,264,1024]{2,1,0:T(8,128)} %get-tuple-element.506, f32[1,256,1024]{2,1,0:T(8,128)S(1)} %dynamic-slice_select_fusion.11, s32[]{:T(128)} %bitcast.169, s32[]{:T(128)} %bitcast.170, s32[]{:T(128)} %constant.18.clone.1..sunk.3) | dynamic-update-slice | bytes 2097156 | tf_op jit(solution)/shard_map/vmap(vmap())/scatter
  310.4 43.6 %reduce-scatter.5.cloned.1.call-done = f32[2,64,1024]{2,1,0:T(8,128)} async-done(((f32[2,256,1024]{2,1,0:T(8,128)}), f32[2,64,1024]{2,1,0:T(8,128)}) %reduce-scatter.5.cloned.1.call-update) | async-done | bytes 524304 | tf_op jit(solution)/shard_map/reduce_scatter | solution.py:96
  356.1 27.2 %all-gather.5.cloned.1.call-done = bf16[2,256,1024]{2,1,0:T(8,128)(2,1)} async-done(((bf16[2,64,1024]{2,1,0:T(8,128)(2,1)}), bf16[2,256,1024]{2,1,0:T(8,128)(2,1)}) %all-gather.5.cloned.1.call-update) | async-done | bytes 1048592 | tf_op jit(solution)/shard_map/all_gather | solution.py:99
  385.2 4.2 fusion.12
  390.0 3.5 add_convert_fusion
  394.9 3.8 collective-permute-done.2
  400.3 8.1 %psum.7 = f32[2]{0:T(128)S(1)} all-reduce(f32[2]{0:T(128)S(1)} %get-tuple-element.189), channel_id=1, replica_groups=mesh['grp'=2,'slab'=4,'ang'=4] {'slab'}, use_global_device_ids=true, to_apply=%region_11.12 | all-reduce | flops 2 | bytes 16 | tf_op jit(solution)/shard_map/psum | solution.py:106
  408.9 37.1 %collective-permute-done.3 = f32[2,256,1024]{2,1,0:T(8,128)} collective-permute-done((f32[2,256,1024]{2,1,0:T(8,128)S(1)}, f32[2,256,1024]{2,1,0:T(8,128)}, u32[]{:S(2)}, u32[]{:S(2)}) %collective-permute-start.3) | collective-permute-done | bytes 2097184 | tf_op jit(solution)/shard_map/ppermute | solution.py:45
  446.1 3.4 subtract_convert_fusion
  (116 shorter events, 48.0 us)
Async XLA Ops:
  7.2 66.7 %copy-start = (f32[2,64,1024]{2,1,0:T(8,128)S(1)}, f32[2,64,1024]{2,1,0:T(8,128)}, u32[]{:S(2)}) copy-start(f32[2,64,1024]{2,1,0:T(8,128)} %param.8) | copy-start | bytes 1572868
  7.2 144.8 %reduce-scatter.3.cloned.1.call-start = ((), (), s32[]{:S(2)}) async-start(), calls=%async_computation.2 | async-start | bytes 2621440 | tf_op jit(solution)/shard_map/reduce_scatter | solution.py:96
  7.2 4.7 %copy-start.4 = (bf16[2,256,1024]{2,1,0:T(8,128)(2,1)S(1)}, bf16[2,256,1024]{2,1,0:T(8,128)(2,1)}, u32[]{:S(2)}) copy-start(bf16[2,256,1024]{2,1,0:T(8,128)(2,1)} %param.5) | copy-start | bytes 3145732
  7.2 4.7 %copy-start.9 = (bf16[2,1024,1024]{2,1,0:T(8,128)(2,1)S(1)}, bf16[2,1024,1024]{2,1,0:T(8,128)(2,1)}, u32[]{:S(2)}) copy-start(bf16[2,1024,1024]{2,1,0:T(8,128)(2,1)} %param.6) | copy-start | bytes 12582916
  11.9 2.6 copy-start.6
  11.9 2.7 copy-start.7
  14.5 1.9 copy-start.5
  65.6 3.0 copy-start.2
  71.6 2.1 copy-start.8
  73.1 110.4 %all-gather.3.cloned.1.call-start = ((), (), s32[]{:S(2)}) async-start(), calls=%async_computation.3 | async-start | bytes 1310720 | tf_op jit(solution)/shard_map/all_gather | solution.py:99
  153.8 200.2 %reduce-scatter.5.cloned.1.call-start = ((), (), s32[]{:S(2)}) async-start(), calls=%async_computation.4 | async-start | bytes 2621440 | tf_op jit(solution)/shard_map/reduce_scatter | solution.py:96
  194.1 5.0 %collective-permute-start = (f32[2,256,1024]{2,1,0:T(8,128)S(1)}, f32[2,256,1024]{2,1,0:T(8,128)S(1)}, u32[]{:S(2)}, u32[]{:S(2)}) collective-permute-start(f32[2,256,1024]{2,1,0:T(8,128)S(1)} %convert_element_type.65), channel_id=1, source_target_pairs={{0,1},{1,0},{2,3},{3,2},{4,5},{5,4},{6,7},{7,6},{8,9},{9,8},{10,11... | collective-permute-start | bytes 6291464 | tf_op jit(solution)/shard_map/ppermute | solution.py:45
  199.4 47.0 %collective-permute-start.1 = (f32[2,256,1024]{2,1,0:T(8,128)S(1)}, f32[2,256,1024]{2,1,0:T(8,128)}, u32[]{:S(2)}, u32[]{:S(2)}) collective-permute-start(f32[2,256,1024]{2,1,0:T(8,128)S(1)} %convert_add_fusion.1), channel_id=1, source_target_pairs={{0,2},{1,3},{2,0},{3,1},{4,6},{5,7},{6,4},{7,5},{8,10},{9,11},{10,... | collective-permute-start | bytes 6291464 | tf_op jit(solution)/shard_map/ppermute | solution.py:45
  200.7 48.2 %copy-start.10 = (bf16[2,1024,1024]{2,1,0:T(8,128)(2,1)S(1)}, bf16[2,1024,1024]{2,1,0:T(8,128)(2,1)}, u32[]{:S(2)}) copy-start(bf16[2,1024,1024]{2,1,0:T(8,128)(2,1)} %param.6) | copy-start | bytes 12582916
  248.9 2.6 copy-start.3
  310.3 73.0 %all-gather.5.cloned.1.call-start = ((), (), s32[]{:S(2)}) async-start(), calls=%async_computation.5 | async-start | bytes 1310720 | tf_op jit(solution)/shard_map/all_gather | solution.py:99
  393.7 5.0 %collective-permute-start.2 = (f32[2,256,1024]{2,1,0:T(8,128)S(1)}, f32[2,256,1024]{2,1,0:T(8,128)S(1)}, u32[]{:S(2)}, u32[]{:S(2)}) collective-permute-start(f32[2,256,1024]{2,1,0:T(8,128)S(1)} %convert_element_type.71), channel_id=1, source_target_pairs={{0,1},{1,0},{2,3},{3,2},{4,5},{5,4},{6,7},{7,6},{8,9},{9,8},{10,11... | collective-permute-start | bytes 6291464 | tf_op jit(solution)/shard_map/ppermute | solution.py:45
  399.1 47.0 %collective-permute-start.3 = (f32[2,256,1024]{2,1,0:T(8,128)S(1)}, f32[2,256,1024]{2,1,0:T(8,128)}, u32[]{:S(2)}, u32[]{:S(2)}) collective-permute-start(f32[2,256,1024]{2,1,0:T(8,128)S(1)} %convert_add_fusion), channel_id=1, source_target_pairs={{0,2},{1,3},{2,0},{3,1},{4,6},{5,7},{6,4},{7,5},{8,10},{9,11},{10,... | collective-permute-start | bytes 6291464 | tf_op jit(solution)/shard_map/ppermute | solution.py:45
  408.4 41.1 %copy-start.1 = (f32[2,64,1024]{2,1,0:T(8,128)S(1)}, f32[2,64,1024]{2,1,0:T(8,128)}, u32[]{:S(2)}) copy-start(f32[2,64,1024]{2,1,0:T(8,128)} %param.8) | copy-start | bytes 1572868
Sparse Core Ops, SparseCore 0:
  73.2 45.2 reduce-scatter.2
  153.9 29.5 all-gather.2
  310.5 43.4 reduce-scatter.4
  356.2 27.0 all-gather.4
